TPU v7x, 1024 devices: a whole 8x8x8 slice. The times are simulated.
1024 devices in a mesh: dp: 16 (over x, core), group: 64 (over z, y).
Axes of the slice: x: 8, y: 8, z: 8, core: 2. Of those that a mesh axis runs over, the one named last changes fastest.
Arguments:
- acts: bfloat16 [2048, 16384], P('dp', 'group'), may hold values from -6 to 6
- cotan: bfloat16 [2048, 8192], P('dp'), may hold values from -0.1875 to 0.1875
- stats: float32 [16, 64, 512, 512], P('dp', 'group'), as said below
- roots: bfloat16 [16, 64, 512, 512], P('dp', 'group'), as said below
- owner: int32 [64], replicated, may hold values from 0 to 63, as said below
- task_of: int32 [64], replicated, may hold values from 0 to 63, as said below
- counts: int32 [64], replicated, may hold values from 1 to 2
Outputs:
- update: bfloat16 [8192, 16384], P('dp', 'group')
- new_stats: float32 [16, 64, 512, 512], P('dp', 'group')
- new_roots: bfloat16 [16, 64, 512, 512], P('dp', 'group')
Inputs may be any that keep to these rules, and one draw needn't show every extreme that they name: A permutation; owner[t] is the group index of the device that keeps task t's statistic; task t is the left (t even) or right (t odd) factor of the block whose columns are held by group indices t - t % 2 and t - t % 2 + 1. `task_of`: the inverse permutation of owner. Each stats[k, o] is symmetric positive definite. Each roots[k, t] is symmetric.
All inputs are finite; a program needn't handle non-finite values.
Results may differ from a plain program's by a relative error of at most 0.0055.
The roundings to bfloat16 on the way count: a program that leaves them out, or rounds other values in their place, can miss the bound.
Values may be sent and summed in bfloat16 or wider, within the bound.
No kernel may reach another device: no remote copies, remote signals or barrier semaphores. Data moves between devices by JAX's collectives and lax.ppermute only.
A program may use at most 128 MiB of HBM per device.

v0:
```python
import jax
import jax.numpy as jnp
from jax import lax
from jax.sharding import PartitionSpec as P

decay_rate = 0.9
ridge = 0.001
highest = lax.Precision.HIGHEST


def swapped(x, axis, distance):
    return lax.ppermute(x, axis, [(i, i ^ 1 << distance) for i in range(lax.axis_size(axis))])


def newton_root(statistic, turns):
    identity = jnp.eye(statistic.shape[0], dtype=jnp.float32)
    matrix = statistic + ridge * identity
    frobenius = jnp.sqrt(jnp.sum(matrix * matrix))
    scaled = matrix / frobenius
    step_matrix = (5.0 * identity - scaled) / 4.0
    root_now = step_matrix * frobenius ** (-0.25)

    def one_turn(index, current_state):
        root_now, scaled, step_matrix = current_state
        squared = jnp.dot(step_matrix, step_matrix, precision=highest)
        scaled = jnp.dot(squared, jnp.dot(squared, scaled, precision=highest), precision=highest)
        step_matrix = (5.0 * identity - scaled) / 4.0
        root_now = jnp.dot(root_now, step_matrix, precision=highest)
        return (root_now, scaled, step_matrix)

    return lax.fori_loop(1, turns, one_turn, (root_now, scaled, step_matrix))[0]


def route_blocks(payload, sources, groups):
    order_size, column_count = payload.shape
    strip_rows = order_size // groups
    spread_out = payload.reshape(groups, strip_rows, column_count)
    middle = lax.all_to_all(spread_out, "group", split_axis=0, concat_axis=0, tiled=True)
    chosen = middle[sources]
    arrived = lax.all_to_all(chosen, "group", split_axis=1, concat_axis=1, tiled=True)
    return arrived.reshape(sources.shape[0], order_size, column_count)


def per_device(acts, cotan, stats, roots, owner, task_of, counts):
    groups = lax.axis_size("group")
    position = lax.axis_index("group")
    half_cols = acts.shape[1]
    column_half = position % 2
    gradient = lax.psum_scatter(
        lax.dot_general(cotan, acts, (((0,), (0,)), ((), ())), preferred_element_type=jnp.float32),
        "dp",
        scatter_dimension=0,
        tiled=True,
    ).astype(jnp.bfloat16)
    own_root = roots[0, 0]
    other_half, other_root = swapped((gradient, own_root), "group", 0)
    first_half = jnp.where(column_half == 0, gradient, other_half)
    second_half = jnp.where(column_half == 0, other_half, gradient)
    full_block = jnp.concatenate([first_half, second_half], 1)
    left_root = jnp.where(column_half == 0, own_root, other_root)
    right_root = jnp.where(column_half == 0, other_root, own_root)
    left_part = jnp.dot(left_root, full_block, preferred_element_type=jnp.float32).astype(
        jnp.bfloat16
    )
    right_columns = lax.dynamic_slice_in_dim(right_root, column_half * half_cols, half_cols, 1)
    update = jnp.dot(left_part, right_columns, preferred_element_type=jnp.float32).astype(
        jnp.bfloat16
    )
    my_task = task_of[position]
    first_source = 2 * (task_of // 2)
    arrived = route_blocks(gradient, jnp.stack([first_source, first_source + 1]), groups)
    assembled = jnp.concatenate([arrived[0], arrived[1]], 1)
    factor = jnp.where(my_task % 2 == 1, assembled.T, assembled)
    gram_product = lax.dot_general(
        factor, factor, (((1,), (1,)), ((), ())), preferred_element_type=jnp.float32
    )
    refreshed_statistic = decay_rate * stats[0, 0] + gram_product
    fresh_root = newton_root(refreshed_statistic, counts[my_task]).astype(jnp.bfloat16)
    returned = route_blocks(fresh_root, owner[None, :], groups)[0]
    return (update, refreshed_statistic[None, None], returned[None, None])


def solution(mesh):
    return jax.shard_map(
        per_device,
        mesh=mesh,
        in_specs=(
            P("dp", "group"),
            P("dp", None),
            P("dp", "group", None, None),
            P("dp", "group", None, None),
            P(),
            P(),
            P(),
        ),
        out_specs=(P("dp", "group"), P("dp", "group", None, None), P("dp", "group", None, None)),
        check_vma=False,
    )
```

profile of v0, /device:TPU:14, one launch (start us, length us, event | category | flops | bytes accessed | tf_op | source)
XLA Modules:
  0.0 252.8 jit_solution(114721155404022674)
XLA Ops:
  7.2 0.0 copy-start
  7.2 0.0 reduce-scatter.2.cloned.1.call-start
  7.2 1.5 copy-done
  8.8 5.4 %fusion.30 = f32[8192,256]{1,0:T(8,128)} fusion(bf16[128,8192]{1,0:T(8,128)(2,1)S(1)} %copy-done, bf16[128,256]{1,0:T(8,128)(2,1)} %param.9), kind=kOutput, calls=%fused_computation.49 | convolution fusion | flops 536870912 | bytes 10551296 | tf_op jit(solution)/shard_map/dot_general | solution.py:50
  14.1 0.0 copy-start.4
  14.1 0.0 reduce-scatter.2.cloned.1.call-update
  14.1 0.0 copy-start.5
  14.2 84.0 %reduce-scatter.2.cloned.1.call-done = f32[512,256]{1,0:T(8,128)} async-done(((f32[8192,256]{1,0:T(8,128)}), f32[512,256]{1,0:T(8,128)}) %reduce-scatter.2.cloned.1.call-update) | async-done | bytes 524304 | tf_op jit(solution)/shard_map/reduce_scatter | solution.py:49
  98.2 1.8 convert_bitcast_fusion.1
  99.9 13.6 %all-to-all-start = ((bf16[64,8,256]{2,1,0:T(8,128)(2,1)}), bf16[64,8,256]{2,1,0:T(8,128)(2,1)S(1)}, u32[]{:S(2)}, u32[]{:S(2)}) async-start(bf16[64,8,256]{2,1,0:T(8,128)(2,1)} %convert_bitcast_fusion.1), calls=%async_computation.1 | async-start | bytes 524288 | tf_op jit(solution)/shard_map/all_to_all | solution.py:38
  113.5 0.0 copy-done.4
  113.6 0.1 reshape.112
  113.7 14.8 %all-to-all-done = bf16[64,8,256]{2,1,0:T(8,128)(2,1)S(1)} async-done(((bf16[64,8,256]{2,1,0:T(8,128)(2,1)}), bf16[64,8,256]{2,1,0:T(8,128)(2,1)S(1)}, u32[]{:S(2)}, u32[]{:S(2)}) %all-to-all-start) | async-done | bytes 262176 | tf_op jit(solution)/shard_map/all_to_all | solution.py:38
  128.4 0.6 gather_fusion
  129.1 0.8 copy.19
  129.9 5.1 %all-to-all-start.1 = ((bf16[2,64,8,256]{3,2,0,1:T(8,128)(2,1)}), bf16[2,64,8,256]{3,2,0,1:T(8,128)(2,1)S(1)}, u32[]{:S(2)}, u32[]{:S(2)}) async-start(bf16[2,64,8,256]{3,2,0,1:T(8,128)(2,1)} %copy.19), calls=%async_computation.2 | async-start | bytes 1048576 | tf_op jit(solution)/shard_map/all_to_all | solution.py:40
  135.1 0.6 dynamic_slice.10
  138.9 0.0 copy-done.5
  138.9 0.7 dynamic_slice.11
  139.6 14.9 %all-to-all-done.1 = bf16[2,64,8,256]{3,2,0,1:T(8,128)(2,1)S(1)} async-done(((bf16[2,64,8,256]{3,2,0,1:T(8,128)(2,1)}), bf16[2,64,8,256]{3,2,0,1:T(8,128)(2,1)S(1)}, u32[]{:S(2)}, u32[]{:S(2)}) %all-to-all-start.1) | async-done | bytes 524320 | tf_op jit(solution)/shard_map/all_to_all | solution.py:40
  154.6 1.0 copy.20
  155.6 3.6 %multiply_reduce_fusion = (f32[]{:T(128)}, f32[512,512]{1,0:T(8,128)}) fusion(bf16[512,512]{0,1:T(8,128)(2,1)} %copy.20, pred[]{:T(512)S(6)} %eq.20, bf16[512,256]{1,0:T(8,128)(2,1)S(1)} %get-tuple-element.87, bf16[512,256]{1,0:T(8,128)(2,1)S(1)} %get-tuple-element.86, f32[1,1,512,512]{3,2,1,0:T(8,128)} %param.11), kind=kOutput, calls=%fused_computation.11 | convolution fusion | flops 271581184 | bytes 3145733 | tf_op jit(solution)/shard_map/dot_general | solution.py:74
  159.8 2.5 fusion.5
  162.4 2.3 fusion.6
  164.8 2.6 %copy.21 = f32[512,512]{0,1:T(8,128)} copy(f32[512,512]{1,0:T(8,128)} %fusion.6) | data formatting | bytes 2097152
  167.3 0.8 while.15
  168.1 0.0 copy-start.6
  168.2 0.0 copy-start.3
  168.2 2.3 copy.22
  170.4 16.5 %all-to-all-start.2 = ((bf16[64,8,512]{2,1,0:T(8,128)(2,1)}), bf16[64,8,512]{2,1,0:T(8,128)(2,1)S(1)}, u32[]{:S(2)}, u32[]{:S(2)}) async-start(bf16[64,8,512]{2,1,0:T(8,128)(2,1)} %bitcast.26), calls=%async_computation.3 | async-start | bytes 1048576 | tf_op jit(solution)/shard_map/all_to_all | solution.py:38
  187.0 0.0 copy-done.6
  187.0 19.3 %all-to-all-done.2 = bf16[64,8,512]{2,1,0:T(8,128)(2,1)S(1)} async-done(((bf16[64,8,512]{2,1,0:T(8,128)(2,1)}), bf16[64,8,512]{2,1,0:T(8,128)(2,1)S(1)}, u32[]{:S(2)}, u32[]{:S(2)}) %all-to-all-start.2) | async-done | bytes 524320 | tf_op jit(solution)/shard_map/all_to_all | solution.py:38
  206.3 1.4 gather_fusion.1
  207.7 5.0 %all-to-all-start.3 = ((bf16[1,64,8,512]{3,2,0,1:T(8,128)(2,1)}), bf16[1,64,8,512]{3,2,0,1:T(8,128)(2,1)S(1)}, u32[]{:S(2)}, u32[]{:S(2)}) async-start(bf16[1,64,8,512]{3,2,0,1:T(8,128)(2,1)} %bitcast.60), calls=%async_computation.4 | async-start | bytes 1048576 | tf_op jit(solution)/shard_map/all_to_all | solution.py:40
  212.8 3.5 %collective-permute-start = (bf16[512,512]{1,0:T(8,128)(2,1)}, bf16[512,512]{1,0:T(8,128)(2,1)}, u32[]{:S(2)}, u32[]{:S(2)}) collective-permute-start(bf16[512,512]{1,0:T(8,128)(2,1)} %bitcast.63), channel_id=1, source_target_pairs={{0,1},{1,0},{2,3},{3,2},{4,5},{5,4},{6,7},{7,6},{8,9},{9,8},{10,11... | collective-permute-start | bytes 1572872 | tf_op jit(solution)/shard_map/ppermute | solution.py:12
  216.2 0.0 copy-done.3
  216.3 0.7 convert_element_type.15
  217.0 2.4 collective-permute-start.1
  219.4 22.1 %collective-permute-done.1 = bf16[512,256]{1,0:T(8,128)(2,1)S(1)} collective-permute-done((bf16[512,256]{1,0:T(8,128)(2,1)}, bf16[512,256]{1,0:T(8,128)(2,1)S(1)}, u32[]{:S(2)}, u32[]{:S(2)}) %collective-permute-start.1) | collective-permute-done | bytes 262176 | tf_op jit(solution)/shard_map/ppermute | solution.py:12
  241.5 0.9 broadcast_select_fusion.1
  242.4 0.0 collective-permute-done
  242.4 2.8 %fusion.4 = bf16[512,256]{1,0:T(8,128)(2,1)} fusion(bf16[512,256]{1,0:T(8,128)(2,1)} %get-tuple-element.89, bf16[512,256]{1,0:T(8,128)(2,1)} %get-tuple-element.88, bf16[512,512]{1,0:T(8,128)(2,1)} %bitcast.64, bf16[512,512]{1,0:T(8,128)(2,1)} %collective-permute-done, pred[]{:T(512)S(6)} %eq.19, s32[]{:T(128)S(6)} %select_n.76), kind=kOutput, calls=%fused_computation.10 | convolution fusion | flops 404488192 | bytes 2360832 | tf_op jit(solution)/shard_map/dot_general | solution.py:66
  245.1 0.0 all-to-all-done.3
  245.1 0.8 copy.39
  (7 shorter events, 0.1 us)
Async XLA Ops:
  7.2 1.6 copy-start
  7.2 91.0 %reduce-scatter.2.cloned.1.call-start = ((), (), s32[]{:S(2)}) async-start(), calls=%async_computation.5 | async-start | bytes 8912896 | tf_op jit(solution)/shard_map/reduce_scatter | solution.py:49
  14.1 99.4 %copy-start.4 = (s32[64]{0:T(128)S(1)}, s32[64]{0:T(128)}, u32[]{:S(2)}) copy-start(s32[64]{0:T(128)} %param.14) | copy-start | bytes 772
  14.1 124.7 %copy-start.5 = (s32[64]{0:T(128)S(1)}, s32[64]{0:T(128)}, u32[]{:S(2)}) copy-start(s32[64]{0:T(128)} %param.15) | copy-start | bytes 772
  99.9 28.5 %all-to-all-start = ((bf16[64,8,256]{2,1,0:T(8,128)(2,1)}), bf16[64,8,256]{2,1,0:T(8,128)(2,1)S(1)}, u32[]{:S(2)}, u32[]{:S(2)}) async-start(bf16[64,8,256]{2,1,0:T(8,128)(2,1)} %convert_bitcast_fusion.1), calls=%async_computation.1 | async-start | bytes 524288 | tf_op jit(solution)/shard_map/all_to_all | solution.py:38
  129.9 24.6 %all-to-all-start.1 = ((bf16[2,64,8,256]{3,2,0,1:T(8,128)(2,1)}), bf16[2,64,8,256]{3,2,0,1:T(8,128)(2,1)S(1)}, u32[]{:S(2)}, u32[]{:S(2)}) async-start(bf16[2,64,8,256]{3,2,0,1:T(8,128)(2,1)} %copy.19), calls=%async_computation.2 | async-start | bytes 1048576 | tf_op jit(solution)/shard_map/all_to_all | solution.py:40
  168.1 18.8 %copy-start.6 = (s32[64]{0:T(128)S(1)}, s32[64]{0:T(128)}, u32[]{:S(2)}) copy-start(s32[64]{0:T(128)} %param.13) | copy-start | bytes 772
  168.2 48.1 %copy-start.3 = (f32[512,256]{1,0:T(8,128)S(1)}, f32[512,256]{1,0:T(8,128)}, u32[]{:S(2)}) copy-start(f32[512,256]{1,0:T(8,128)} %reduce-scatter.2.cloned.1.call-done) | copy-start | bytes 1572868
  170.4 35.9 %all-to-all-start.2 = ((bf16[64,8,512]{2,1,0:T(8,128)(2,1)}), bf16[64,8,512]{2,1,0:T(8,128)(2,1)S(1)}, u32[]{:S(2)}, u32[]{:S(2)}) async-start(bf16[64,8,512]{2,1,0:T(8,128)(2,1)} %bitcast.26), calls=%async_computation.3 | async-start | bytes 1048576 | tf_op jit(solution)/shard_map/all_to_all | solution.py:38
  207.7 37.4 %all-to-all-start.3 = ((bf16[1,64,8,512]{3,2,0,1:T(8,128)(2,1)}), bf16[1,64,8,512]{3,2,0,1:T(8,128)(2,1)S(1)}, u32[]{:S(2)}, u32[]{:S(2)}) async-start(bf16[1,64,8,512]{3,2,0,1:T(8,128)(2,1)} %bitcast.60), calls=%async_computation.4 | async-start | bytes 1048576 | tf_op jit(solution)/shard_map/all_to_all | solution.py:40
  212.8 29.6 %collective-permute-start = (bf16[512,512]{1,0:T(8,128)(2,1)}, bf16[512,512]{1,0:T(8,128)(2,1)}, u32[]{:S(2)}, u32[]{:S(2)}) collective-permute-start(bf16[512,512]{1,0:T(8,128)(2,1)} %bitcast.63), channel_id=1, source_target_pairs={{0,1},{1,0},{2,3},{3,2},{4,5},{5,4},{6,7},{7,6},{8,9},{9,8},{10,11... | collective-permute-start | bytes 1572872 | tf_op jit(solution)/shard_map/ppermute | solution.py:12
  217.0 24.5 %collective-permute-start.1 = (bf16[512,256]{1,0:T(8,128)(2,1)}, bf16[512,256]{1,0:T(8,128)(2,1)S(1)}, u32[]{:S(2)}, u32[]{:S(2)}) collective-permute-start(bf16[512,256]{1,0:T(8,128)(2,1)} %convert_element_type.15), channel_id=1, source_target_pairs={{0,1},{1,0},{2,3},{3,2},{4,5},{5,4},{6,7},{7,6},{8,9},{9,8},{10,11... | collective-permute-start | bytes 786440 | tf_op jit(solution)/shard_map/ppermute | solution.py:12
Sparse Core Ops, SparseCore 0:
  14.3 83.8 reduce-scatter.1
where the time goes:
time: 254 us; the launch traced here: 253 us
  waiting for transfers between devices  155 us (61%)
  starting transfers between devices  46.1 us (18%)
  between operations  18.2 us (7%)
  local copies, waits for them, and re-layouts  12.4 us (5%)
  matrix products  11.7 us (5%)
  other arithmetic  8.29 us (3%)
    reduce_scatter x1, waiting for transfers between devices, per_device(): lax.psum_scatter(lax.dot_general(cotan, acts, (((0,), (0,)), ((), ())), p...  84 us
    all_to_all x2, waiting for transfers between devices, route_blocks(): lax.all_to_all(spread_out, 'group', split_axis=0, concat_axis=0, tiled=True)  34.1 us
    all_to_all x2, starting transfers between devices, route_blocks(): lax.all_to_all(spread_out, 'group', split_axis=0, concat_axis=0, tiled=True)  30.1 us
    ppermute x2, waiting for transfers between devices, swapped(): lax.ppermute(x, axis, [(i, i ^ 1 << distance) for i in range(lax.axis_siz...  22.2 us
    all_to_all x2, waiting for transfers between devices, route_blocks(): lax.all_to_all(chosen, 'group', split_axis=1, concat_axis=1, tiled=True)  14.9 us
    all_to_all x2, starting transfers between devices, route_blocks(): lax.all_to_all(chosen, 'group', split_axis=1, concat_axis=1, tiled=True)  10.1 us
    ppermute x2, starting transfers between devices, swapped(): lax.ppermute(x, axis, [(i, i ^ 1 << distance) for i in range(lax.axis_siz...  5.83 us
    dot_general x1, matrix products, per_device(): lax.dot_general(cotan, acts, (((0,), (0,)), ((), ())), preferred_element_...  5.36 us
  transfers between devices with their start and end apart: 7, of which 5 were waited for; matrix products, arithmetic and copies ran while one was open for 2% of the time, Pallas kernels for 0%

commit v1 on v0

v1 whole, which is shorter than its diff:
```python
import jax
import jax.numpy as jnp
from jax import lax
from jax.experimental import pallas as pl
from jax.experimental.pallas import tpu as pltpu
from jax.sharding import PartitionSpec as P

decay_rate = 0.9
ridge = 0.001
BF = jnp.bfloat16
F32 = jnp.float32
LANES = 128
SIDE = 8
PARTS = 4
STAT_ROWS = 24
STRIP = 32


def dot(a, b, dims=((1,), (0,))):
    return lax.dot_general(a, b, (dims, ((), ())), preferred_element_type=F32)


def smem():
    return pl.BlockSpec(memory_space=pltpu.SMEM)


def vmem(count):
    return [pl.BlockSpec(memory_space=pltpu.VMEM)] * count


def strip_tiles(groups):
    half = groups // 2
    low = half * 8
    for a in range(half):
        for strip, place, row, lane in (
            (a, 0, a * 8, 0),
            (a, 1, a * 8, 1),
            (a, 2, low + a * 8, 0),
            (half + a, 0, low + a * 8, 1),
            (half + a, 1, low + a * 8, 2),
            (half + a, 2, low + a * 8, 3),
        ):
            yield strip, place * 8, row, lane * LANES


def pack_kernel(stats, acts, out):
    groups = out.shape[0]
    for strip, place, row, lane in strip_tiles(groups):
        out[strip, place : place + 8, :] = stats[row : row + 8, lane : lane + LANES].astype(BF)
    for tile in range(groups // 2):
        row, lane = tile // 2 * 8, tile % 2 * LANES
        piece = acts[row : row + 8, lane : lane + LANES]
        out[2 * tile, STAT_ROWS:, :] = piece
        out[2 * tile + 1, STAT_ROWS:, :] = piece


def select_kernel(stat_source, act_source, middle, out):
    def one(o, carry):
        out[o, :STAT_ROWS, :] = middle[stat_source[o], :STAT_ROWS, :]
        out[o, STAT_ROWS:, :] = middle[act_source[o], STAT_ROWS:, :]
        return carry

    lax.fori_loop(0, out.shape[0], one, 0, unroll=8)


def acts_kernel(scalars, own, other, arrived, out):
    cols = own.shape[1]
    half = scalars[0]

    @pl.when(half == 0)
    def _():
        out[:, :cols] = own[...]
        out[:, cols : 2 * cols] = other[...]

    @pl.when(half == 1)
    def _():
        out[:, :cols] = other[...]
        out[:, cols : 2 * cols] = own[...]

    for strip in range(arrived.shape[0]):
        tile, side = strip // 2, strip % 2
        row, lane = tile // 2 * 8, 2 * cols + side * cols + tile % 2 * LANES
        out[row : row + 8, lane : lane + LANES] = arrived[strip, STAT_ROWS:, :]


def cotan_kernel(scalars, cotan, out, buffer, sems):
    count = out.shape[0]

    def copy(k):
        start = pl.multiple_of((k * PARTS + scalars[0]) * LANES, LANES)
        return pltpu.make_async_copy(cotan.at[:, pl.ds(start, LANES)], buffer.at[k], sems.at[k])

    for k in range(count):
        copy(k).start()
    for k in range(count):
        copy(k).wait()
        out[k] = buffer[k].T


def gram_into(block, odd, out_ref):
    @pl.when(odd == 0)
    def _():
        out_ref[...] = dot(block, block, ((1,), (1,)))

    @pl.when(odd == 1)
    def _():
        out_ref[...] = dot(block, block, ((0,), (0,)))


def step_kernel(
    scalars,
    part0,
    part1,
    part2,
    part3,
    acts,
    own_root,
    other_root,
    arrived,
    stats,
    update,
    new_stats,
    new_root,
    block,
    gram,
    old,
    root,
):
    half = scalars[0]
    turns = scalars[1]
    kept_odd = scalars[2]
    first_part = scalars[3]
    n = stats.shape[0]
    half_cols = n // 2

    for shift, part in enumerate((part0, part1, part2, part3)):
        rows = jnp.concatenate([part[i] for i in range(part.shape[0])], 1)
        start = pl.multiple_of((first_part + shift) % PARTS * LANES, LANES)
        block[pl.ds(start, LANES), :] = dot(rows, acts[...]).astype(BF)

    kept = block[:, n:]
    gram_into(kept, kept_odd, gram)
    new_stats[...] = decay_rate * stats[...] + gram[...]

    own = block[:, :n]

    @pl.when(half == 0)
    def _():
        left_part = dot(own_root[...], own).astype(BF)
        update[...] = dot(left_part, other_root[:, :half_cols]).astype(BF)

    @pl.when(half == 1)
    def _():
        left_part = dot(other_root[...], own).astype(BF)
        update[...] = dot(left_part, own_root[:, half_cols:]).astype(BF)

    for strip, place, row, lane in strip_tiles(arrived.shape[0]):
        old[row : row + 8, lane : lane + LANES] = arrived[strip, place : place + 8, :].astype(F32)
    old[:half_cols, half_cols:] = old[half_cols:, :half_cols].T

    gram_into(own, half, gram)
    identity = (
        lax.broadcasted_iota(jnp.int32, (n, n), 0) == lax.broadcasted_iota(jnp.int32, (n, n), 1)
    ).astype(F32)
    matrix = decay_rate * old[...] + gram[...] + ridge * identity
    square_sum = jnp.sum(jnp.sum(matrix * matrix, axis=0, keepdims=True), axis=1, keepdims=True)
    inv_norm = lax.rsqrt(square_sum)
    scaled = matrix * inv_norm
    gram[...] = scaled
    root[...] = jnp.sqrt(jnp.sqrt(inv_norm)) * (1.25 * identity - 0.25 * scaled)

    def one_turn(_, carry):
        m = gram[...]
        mb = m.astype(BF)
        q = ((dot(mb, mb) - 10.0 * m) * 0.0625).astype(BF)
        t = 1.5625 * m + dot(q, mb)
        m = 1.5625 * t + dot(q, t.astype(BF))
        gram[...] = m
        x = root[...]
        root[...] = 1.25 * x - 0.25 * dot(x.astype(BF), m.astype(BF))
        return carry

    lax.fori_loop(1, turns, one_turn, 0)
    new_root[...] = root[...].astype(BF)


def from_partner(x, partner):
    count = lax.axis_size("group")
    return lax.ppermute(x, "group", [(partner(i), i) for i in range(count)])


def z_up(i):
    return (i + SIDE) % (SIDE * SIDE)


def z_down(i):
    return (i - SIDE) % (SIDE * SIDE)


def y_outer(i):
    y = i % SIDE
    return i - y + (y + (1 if y % 2 else -1)) % SIDE


def pair(i):
    return i ^ 1


def per_device(acts, cotan, stats, roots, owner, task_of, counts):
    groups = lax.axis_size("group")
    rows = lax.axis_size("dp")
    position = lax.axis_index("group")
    n = stats.shape[-1]
    half = position % 2
    my_task = task_of[position]
    old_stats = stats[0, 0]
    own_root = roots[0, 0]

    strips = pl.pallas_call(
        pack_kernel,
        out_shape=jax.ShapeDtypeStruct((groups, STRIP, LANES), BF),
        in_specs=vmem(2),
        out_specs=vmem(1)[0],
        name="pack_strips",
    )(old_stats, acts)
    middle = lax.all_to_all(strips, "group", split_axis=0, concat_axis=0, tiled=True)
    chosen = pl.pallas_call(
        select_kernel,
        out_shape=jax.ShapeDtypeStruct((groups, STRIP, LANES), BF),
        in_specs=[smem(), smem()] + vmem(1),
        out_specs=vmem(1)[0],
        name="select_strips",
    )(owner, task_of // 2 * 2 + half, middle)
    arrived = lax.all_to_all(chosen, "group", split_axis=0, concat_axis=0, tiled=True)

    other_acts = from_partner(acts, pair)
    both_acts = pl.pallas_call(
        acts_kernel,
        out_shape=jax.ShapeDtypeStruct((acts.shape[0], 2 * n), BF),
        in_specs=[smem()] + vmem(3),
        out_specs=vmem(1)[0],
        name="join_acts",
    )(jnp.reshape(half, (1,)), acts, other_acts, arrived)
    all_acts = lax.all_gather(both_acts, "dp", axis=0, tiled=True)

    first_part = (position // SIDE + 2 * (position % SIDE)) % PARTS
    tokens = cotan.shape[0]
    part = pl.pallas_call(
        cotan_kernel,
        out_shape=jax.ShapeDtypeStruct((rows, LANES, tokens), BF),
        in_specs=[smem(), pl.BlockSpec(memory_space=pl.ANY)],
        out_specs=vmem(1)[0],
        scratch_shapes=[pltpu.VMEM((rows, tokens, LANES), BF), pltpu.SemaphoreType.DMA((rows,))],
        name="cotan_part",
    )(jnp.reshape(first_part, (1,)), cotan)
    part0 = lax.all_to_all(part, "dp", split_axis=0, concat_axis=0, tiled=True)
    part1 = from_partner(part0, z_up)
    part2 = from_partner(part0, y_outer)
    part3 = from_partner(part0, z_down)

    other_root = from_partner(own_root, pair)

    update, new_stats, new_root = pl.pallas_call(
        step_kernel,
        out_shape=(
            jax.ShapeDtypeStruct((n, n // 2), BF),
            jax.ShapeDtypeStruct((n, n), F32),
            jax.ShapeDtypeStruct((n, n), BF),
        ),
        in_specs=[smem()] + vmem(9),
        out_specs=tuple(vmem(3)),
        scratch_shapes=[
            pltpu.VMEM((n, 2 * n), BF),
            pltpu.VMEM((n, n), F32),
            pltpu.VMEM((n, n), F32),
            pltpu.VMEM((n, n), F32),
        ],
        name="shampoo_step",
    )(
        jnp.stack([half, counts[position], my_task % 2, first_part]),
        part0,
        part1,
        part2,
        part3,
        all_acts,
        own_root,
        other_root,
        arrived,
        old_stats,
    )
    return (update, new_stats[None, None], new_root[None, None])


def solution(mesh):
    return jax.shard_map(
        per_device,
        mesh=mesh,
        in_specs=(
            P("dp", "group"),
            P("dp", None),
            P("dp", "group", None, None),
            P("dp", "group", None, None),
            P(),
            P(),
            P(),
        ),
        out_specs=(P("dp", "group"), P("dp", "group", None, None), P("dp", "group", None, None)),
        check_vma=False,
    )
```

time: 254 us -> 155 us (0.61)
  the two profiles are of different devices: /device:TPU:14 before, /device:TPU:1 now
where the time goes in v1:
time: 155 us; the launch traced here: 154 us
  starting transfers between devices  57.3 us (37%)
  waiting for transfers between devices  56.2 us (36%)
  Pallas kernels  18.6 us (12%)
  between operations  16.2 us (10%)
  local copies, waits for them, and re-layouts  3.59 us (2%)
  other arithmetic  2.45 us (2%)
    all_to_all x1, starting transfers between devices, per_device(): lax.all_to_all(strips, 'group', split_axis=0, concat_axis=0, tiled=True)  24.1 us
    all_to_all x1, waiting for transfers between devices, per_device(): part0 = lax.all_to_all(part, 'dp', split_axis=0, concat_axis=0, tiled=True)  18.8 us
    ppermute x5, waiting for transfers between devices, from_partner(): return lax.ppermute(x, 'group', [(partner(i), i) for i in range(count)])  17.6 us
    all_to_all x1, waiting for transfers between devices, per_device(): lax.all_to_all(strips, 'group', split_axis=0, concat_axis=0, tiled=True)  16.2 us
    ppermute x5, starting transfers between devices, from_partner(): return lax.ppermute(x, 'group', [(partner(i), i) for i in range(count)])  15.4 us
    all_to_all x1, starting transfers between devices, per_device(): part0 = lax.all_to_all(part, 'dp', split_axis=0, concat_axis=0, tiled=True)  11.1 us
    pallas_call x1, Pallas kernels, per_device(): pl.pallas_call(step_kernel, out_shape=(jax.ShapeDtypeStruct((n, n // 2),...  9.74 us
    all_to_all x1, starting transfers between devices, per_device(): lax.all_to_all(chosen, 'group', split_axis=0, concat_axis=0, tiled=True)  6.7 us
  transfers between devices with their start and end apart: 9, of which 7 were waited for; matrix products, arithmetic and copies ran while one was open for 2% of the time, Pallas kernels for 2%

profile of v1, /device:TPU:1, one launch (start us, length us, event | category | flops | bytes accessed | tf_op | source)
XLA Modules:
  0.0 154.3 jit_solution(1753471257045608883)
XLA Ops:
  7.2 0.0 copy-start.8
  7.2 2.1 %pack_strips.1 = bf16[64,32,128]{2,1,0:T(8,128)(2,1)} custom-call(f32[512,512]{1,0:T(8,128)} %bitcast.8, bf16[128,256]{1,0:T(8,128)(2,1)} %own.1), custom_call_target="tpu_custom_call" | custom-call | tf_op jit(solution)/shard_map/pack_strips/pallas_call | solution.py:219
  9.3 0.0 copy-start.3
  9.3 0.0 copy-start.10
  9.3 0.0 copy-start.11
  9.3 24.1 %all-to-all-start.1 = ((bf16[64,32,128]{2,1,0:T(8,128)(2,1)}), bf16[64,32,128]{2,1,0:T(8,128)(2,1)S(1)}, u32[]{:S(2)}, u32[]{:S(2)}) async-start(bf16[64,32,128]{2,1,0:T(8,128)(2,1)} %pack_strips.1), calls=%async_computation.1 | async-start | bytes 1048576 | tf_op jit(solution)/shard_map/all_to_all | solution.py:226
  33.4 1.2 multiply_add_fusion.act_source
  34.6 16.2 %all-to-all-done.1.middle = bf16[64,32,128]{2,1,0:T(8,128)(2,1)S(1)} async-done(((bf16[64,32,128]{2,1,0:T(8,128)(2,1)}), bf16[64,32,128]{2,1,0:T(8,128)(2,1)S(1)}, u32[]{:S(2)}, u32[]{:S(2)}) %all-to-all-start.1) | async-done | bytes 524320 | tf_op jit(solution)/shard_map/all_to_all | solution.py:226
  50.8 0.0 copy-start.2
  50.8 0.8 copy-done.2
  51.6 2.0 %select_strips.1 = bf16[64,32,128]{2,1,0:T(8,128)(2,1)} custom-call(s32[64]{0:T(128)} %stat_source.1, s32[64]{0:T(128)} %multiply_add_fusion.act_source, bf16[64,32,128]{2,1,0:T(8,128)(2,1)} %copy-done.2), custom_call_target="tpu_custom_call" | custom-call | tf_op jit(solution)/shard_map/select_strips/pallas_call | solution.py:227
  53.6 6.7 %all-to-all-start.2 = ((bf16[64,32,128]{2,1,0:T(8,128)(2,1)}), bf16[64,32,128]{2,1,0:T(8,128)(2,1)S(1)}, u32[]{:S(2)}, u32[]{:S(2)}) async-start(bf16[64,32,128]{2,1,0:T(8,128)(2,1)} %select_strips.1), calls=%async_computation.2 | async-start | bytes 1048576 | tf_op jit(solution)/shard_map/all_to_all | solution.py:234
  60.3 0.0 all-gather.2.cloned.1.call-start
  60.4 0.0 copy-done.8
  60.4 2.9 %collective-permute-start.3 = (bf16[128,256]{1,0:T(8,128)(2,1)S(1)}, bf16[128,256]{1,0:T(8,128)(2,1)S(1)}, u32[]{:S(2)}, u32[]{:S(2)}) collective-permute-start(bf16[128,256]{1,0:T(8,128)(2,1)S(1)} %copy-done.8), channel_id=1, source_target_pairs={{1,0},{0,1},{3,2},{2,3},{5,4},{4,5},{7,6},{6,7},{9,8},{8,9},{11,10... | collective-permute-start | bytes 196616 | tf_op jit(solution)/shard_map/ppermute | solution.py:189
  63.3 10.1 %collective-permute-done.3.other = bf16[128,256]{1,0:T(8,128)(2,1)S(1)} collective-permute-done((bf16[128,256]{1,0:T(8,128)(2,1)S(1)}, bf16[128,256]{1,0:T(8,128)(2,1)S(1)}, u32[]{:S(2)}, u32[]{:S(2)}) %collective-permute-start.3) | collective-permute-done | bytes 65568 | tf_op jit(solution)/shard_map/ppermute | solution.py:189
  73.4 0.0 copy-start.9
  73.4 3.5 %all-to-all-done.2.arrived = bf16[64,32,128]{2,1,0:T(8,128)(2,1)S(1)} async-done(((bf16[64,32,128]{2,1,0:T(8,128)(2,1)}), bf16[64,32,128]{2,1,0:T(8,128)(2,1)S(1)}, u32[]{:S(2)}, u32[]{:S(2)}) %all-to-all-start.2) | async-done | bytes 524320 | tf_op jit(solution)/shard_map/all_to_all | solution.py:234
  76.9 0.0 copy-start
  76.9 0.0 copy-done.9
  76.9 0.8 copy-done
  77.7 1.9 %join_acts.1 = bf16[128,1024]{1,0:T(8,128)(2,1)} custom-call(s32[1]{0:T(128)} %bitcast.scalars, bf16[128,256]{1,0:T(8,128)(2,1)} %own.1, bf16[128,256]{1,0:T(8,128)(2,1)} %copy-done.9, bf16[64,32,128]{2,1,0:T(8,128)(2,1)} %copy-done), custom_call_target="tpu_custom_call" | custom-call | tf_op jit(solution)/shard_map/join_acts/pallas_call | solution.py:237
  79.6 0.0 all-gather.2.cloned.1.call-update
  79.7 2.8 %cotan_part.1 = bf16[16,128,128]{2,1,0:T(8,128)(2,1)} custom-call(s32[1]{0:T(128)} %bitcast.3.scalars, bf16[128,8192]{1,0:T(8,128)(2,1)} %cotan.1), custom_call_target="tpu_custom_call" | custom-call | tf_op jit(solution)/shard_map/cotan_part/pallas_call | solution.py:248
  82.5 11.1 %all-to-all-start = ((bf16[16,128,128]{2,1,0:T(8,128)(2,1)}), bf16[16,128,128]{2,1,0:T(8,128)(2,1)S(1)}, u32[]{:S(2)}, u32[]{:S(2)}) async-start(bf16[16,128,128]{2,1,0:T(8,128)(2,1)} %cotan_part.1), calls=%async_computation | async-start | bytes 1048576 | tf_op jit(solution)/shard_map/all_to_all | solution.py:256
  93.7 0.0 copy-done.3
  93.7 3.3 %collective-permute-start.4 = (bf16[512,512]{1,0:T(8,128)(2,1)S(1)}, bf16[512,512]{1,0:T(8,128)(2,1)S(1)}, u32[]{:S(2)}, u32[]{:S(2)}) collective-permute-start(bf16[512,512]{1,0:T(8,128)(2,1)S(1)} %bitcast.11), channel_id=1, source_target_pairs={{1,0},{0,1},{3,2},{2,3},{5,4},{4,5},{7,6},{6,7},{9,8},{8,9},{11,10... | collective-permute-start | bytes 1572872 | tf_op jit(solution)/shard_map/ppermute | solution.py:189
  96.9 18.8 %all-to-all-done.part0 = bf16[16,128,128]{2,1,0:T(8,128)(2,1)S(1)} async-done(((bf16[16,128,128]{2,1,0:T(8,128)(2,1)}), bf16[16,128,128]{2,1,0:T(8,128)(2,1)S(1)}, u32[]{:S(2)}, u32[]{:S(2)}) %all-to-all-start) | async-done | bytes 524320 | tf_op jit(solution)/shard_map/all_to_all | solution.py:256
  115.7 0.0 copy-start.1
  115.7 2.4 %collective-permute-start.2 = (bf16[16,128,128]{2,1,0:T(8,128)(2,1)S(1)}, bf16[16,128,128]{2,1,0:T(8,128)(2,1)S(1)}, u32[]{:S(2)}, u32[]{:S(2)}) collective-permute-start(bf16[16,128,128]{2,1,0:T(8,128)(2,1)S(1)} %all-to-all-done.part0), channel_id=1, source_target_pairs={{56,0},{57,1},{58,2},{59,3},{60,4},{61,5},{62,6},{63,7},{0,8},{1,9... | collective-permute-start | bytes 1572872 | tf_op jit(solution)/shard_map/ppermute | solution.py:189
  118.1 3.8 %collective-permute-start.1 = (bf16[16,128,128]{2,1,0:T(8,128)(2,1)S(1)}, bf16[16,128,128]{2,1,0:T(8,128)(2,1)S(1)}, u32[]{:S(2)}, u32[]{:S(2)}) collective-permute-start(bf16[16,128,128]{2,1,0:T(8,128)(2,1)S(1)} %all-to-all-done.part0), channel_id=1, source_target_pairs={{7,0},{2,1},{1,2},{4,3},{3,4},{6,5},{5,6},{0,7},{15,8},{10,9},{9,1... | collective-permute-start | bytes 1572872 | tf_op jit(solution)/shard_map/ppermute | solution.py:189
  121.9 3.0 %collective-permute-start = (bf16[16,128,128]{2,1,0:T(8,128)(2,1)S(1)}, bf16[16,128,128]{2,1,0:T(8,128)(2,1)S(1)}, u32[]{:S(2)}, u32[]{:S(2)}) collective-permute-start(bf16[16,128,128]{2,1,0:T(8,128)(2,1)S(1)} %all-to-all-done.part0), channel_id=1, source_target_pairs={{8,0},{9,1},{10,2},{11,3},{12,4},{13,5},{14,6},{15,7},{16,8},{17,9... | collective-permute-start | bytes 1572872 | tf_op jit(solution)/shard_map/ppermute | solution.py:189
  124.9 0.0 copy-done.10
  124.9 0.6 dynamic_slice.7
  127.5 0.0 copy-done.11
  127.5 0.6 dynamic_slice.6
  128.1 1.3 pad_add_fusion.scalars
  129.4 0.0 collective-permute-done.4.other_root
  129.4 0.0 copy-start.4
  129.4 3.0 %collective-permute-done.2.part3 = bf16[16,128,128]{2,1,0:T(8,128)(2,1)S(1)} collective-permute-done((bf16[16,128,128]{2,1,0:T(8,128)(2,1)S(1)}, bf16[16,128,128]{2,1,0:T(8,128)(2,1)S(1)}, u32[]{:S(2)}, u32[]{:S(2)}) %collective-permute-start.2) | collective-permute-done | bytes 524320 | tf_op jit(solution)/shard_map/ppermute | solution.py:189
  132.4 0.0 copy-start.5
  132.4 2.5 %collective-permute-done.1.part2 = bf16[16,128,128]{2,1,0:T(8,128)(2,1)S(1)} collective-permute-done((bf16[16,128,128]{2,1,0:T(8,128)(2,1)S(1)}, bf16[16,128,128]{2,1,0:T(8,128)(2,1)S(1)}, u32[]{:S(2)}, u32[]{:S(2)}) %collective-permute-start.1) | collective-permute-done | bytes 524320 | tf_op jit(solution)/shard_map/ppermute | solution.py:189
  134.9 0.0 copy-start.6
  134.9 2.0 %collective-permute-done.part1 = bf16[16,128,128]{2,1,0:T(8,128)(2,1)S(1)} collective-permute-done((bf16[16,128,128]{2,1,0:T(8,128)(2,1)S(1)}, bf16[16,128,128]{2,1,0:T(8,128)(2,1)S(1)}, u32[]{:S(2)}, u32[]{:S(2)}) %collective-permute-start) | collective-permute-done | bytes 524320 | tf_op jit(solution)/shard_map/ppermute | solution.py:189
  136.9 0.0 copy-start.7
  136.9 0.0 all-gather.2.cloned.1.call-done.acts
  136.9 0.0 copy-done.1
  136.9 0.0 copy-done.4
  136.9 0.0 copy-done.5
  136.9 0.0 copy-done.6
  136.9 0.8 copy-done.7
  137.7 9.7 %shampoo_step.1 = (bf16[512,256]{1,0:T(8,128)(2,1)}, f32[512,512]{1,0:T(8,128)}, bf16[512,512]{1,0:T(8,128)(2,1)}) custom-call(s32[4]{0:T(128)} %pad_add_fusion.scalars, bf16[16,128,128]{2,1,0:T(8,128)(2,1)} %copy-done.1, bf16[16,128,128]{2,1,0:T(8,128)(2,1)} %copy-done.7, bf16[16,128,128]{2,1,0:T(8,128)(2,1)} %copy-done.6, bf16[16,128,128]{2,1,0:T(8,128)(2,1)} %copy-done.5, ...), custom_call_target="tpu_custom_call" | custom-call | tf_op jit(solution)/shard_map/shampoo_step/pallas_call | solution.py:263
Async XLA Ops:
  7.2 53.2 %copy-start.8 = (bf16[128,256]{1,0:T(8,128)(2,1)S(1)}, bf16[128,256]{1,0:T(8,128)(2,1)}, u32[]{:S(2)}) copy-start(bf16[128,256]{1,0:T(8,128)(2,1)} %own.1) | copy-start | bytes 196612
  9.3 84.4 %copy-start.3 = (bf16[1,1,512,512]{3,2,1,0:T(8,128)(2,1)S(1)}, bf16[1,1,512,512]{3,2,1,0:T(8,128)(2,1)}, u32[]{:S(2)}) copy-start(bf16[1,1,512,512]{3,2,1,0:T(8,128)(2,1)} %param.10) | copy-start | bytes 1572868
  9.3 115.6 %copy-start.10 = (s32[64]{0:T(128)S(1)}, s32[64]{0:T(128)}, u32[]{:S(2)}) copy-start(s32[64]{0:T(128)} %param.12) | copy-start | bytes 772
  9.3 118.2 %copy-start.11 = (s32[64]{0:T(128)S(1)}, s32[64]{0:T(128)}, u32[]{:S(2)}) copy-start(s32[64]{0:T(128)} %param.13) | copy-start | bytes 772
  9.3 41.5 %all-to-all-start.1 = ((bf16[64,32,128]{2,1,0:T(8,128)(2,1)}), bf16[64,32,128]{2,1,0:T(8,128)(2,1)S(1)}, u32[]{:S(2)}, u32[]{:S(2)}) async-start(bf16[64,32,128]{2,1,0:T(8,128)(2,1)} %pack_strips.1), calls=%async_computation.1 | async-start | bytes 1048576 | tf_op jit(solution)/shard_map/all_to_all | solution.py:226
  50.8 0.8 copy-start.2
  53.6 23.3 %all-to-all-start.2 = ((bf16[64,32,128]{2,1,0:T(8,128)(2,1)}), bf16[64,32,128]{2,1,0:T(8,128)(2,1)S(1)}, u32[]{:S(2)}, u32[]{:S(2)}) async-start(bf16[64,32,128]{2,1,0:T(8,128)(2,1)} %select_strips.1), calls=%async_computation.2 | async-start | bytes 1048576 | tf_op jit(solution)/shard_map/all_to_all | solution.py:234
  60.3 76.6 %all-gather.2.cloned.1.call-start = ((), (), s32[]{:S(2)}) async-start(), calls=%async_computation.3 | async-start | bytes 4456448 | tf_op jit(solution)/shard_map/all_gather | solution.py:244
  60.4 13.1 %collective-permute-start.3 = (bf16[128,256]{1,0:T(8,128)(2,1)S(1)}, bf16[128,256]{1,0:T(8,128)(2,1)S(1)}, u32[]{:S(2)}, u32[]{:S(2)}) collective-permute-start(bf16[128,256]{1,0:T(8,128)(2,1)S(1)} %copy-done.8), channel_id=1, source_target_pairs={{1,0},{0,1},{3,2},{2,3},{5,4},{4,5},{7,6},{6,7},{9,8},{8,9},{11,10... | collective-permute-start | bytes 196616 | tf_op jit(solution)/shard_map/ppermute | solution.py:189
  73.4 3.5 %copy-start.9 = (bf16[128,256]{1,0:T(8,128)(2,1)}, bf16[128,256]{1,0:T(8,128)(2,1)S(1)}, u32[]{:S(2)}) copy-start(bf16[128,256]{1,0:T(8,128)(2,1)S(1)} %collective-permute-done.3.other) | copy-start | bytes 196612
  76.9 0.8 copy-start
  82.5 33.2 %all-to-all-start = ((bf16[16,128,128]{2,1,0:T(8,128)(2,1)}), bf16[16,128,128]{2,1,0:T(8,128)(2,1)S(1)}, u32[]{:S(2)}, u32[]{:S(2)}) async-start(bf16[16,128,128]{2,1,0:T(8,128)(2,1)} %cotan_part.1), calls=%async_computation | async-start | bytes 1048576 | tf_op jit(solution)/shard_map/all_to_all | solution.py:256
  93.7 35.7 %collective-permute-start.4 = (bf16[512,512]{1,0:T(8,128)(2,1)S(1)}, bf16[512,512]{1,0:T(8,128)(2,1)S(1)}, u32[]{:S(2)}, u32[]{:S(2)}) collective-permute-start(bf16[512,512]{1,0:T(8,128)(2,1)S(1)} %bitcast.11), channel_id=1, source_target_pairs={{1,0},{0,1},{3,2},{2,3},{5,4},{4,5},{7,6},{6,7},{9,8},{8,9},{11,10... | collective-permute-start | bytes 1572872 | tf_op jit(solution)/shard_map/ppermute | solution.py:189
  115.7 21.2 %copy-start.1 = (bf16[16,128,128]{2,1,0:T(8,128)(2,1)}, bf16[16,128,128]{2,1,0:T(8,128)(2,1)S(1)}, u32[]{:S(2)}) copy-start(bf16[16,128,128]{2,1,0:T(8,128)(2,1)S(1)} %all-to-all-done.part0) | copy-start | bytes 1572868
  115.7 16.7 %collective-permute-start.2 = (bf16[16,128,128]{2,1,0:T(8,128)(2,1)S(1)}, bf16[16,128,128]{2,1,0:T(8,128)(2,1)S(1)}, u32[]{:S(2)}, u32[]{:S(2)}) collective-permute-start(bf16[16,128,128]{2,1,0:T(8,128)(2,1)S(1)} %all-to-all-done.part0), channel_id=1, source_target_pairs={{56,0},{57,1},{58,2},{59,3},{60,4},{61,5},{62,6},{63,7},{0,8},{1,9... | collective-permute-start | bytes 1572872 | tf_op jit(solution)/shard_map/ppermute | solution.py:189
  118.1 16.8 %collective-permute-start.1 = (bf16[16,128,128]{2,1,0:T(8,128)(2,1)S(1)}, bf16[16,128,128]{2,1,0:T(8,128)(2,1)S(1)}, u32[]{:S(2)}, u32[]{:S(2)}) collective-permute-start(bf16[16,128,128]{2,1,0:T(8,128)(2,1)S(1)} %all-to-all-done.part0), channel_id=1, source_target_pairs={{7,0},{2,1},{1,2},{4,3},{3,4},{6,5},{5,6},{0,7},{15,8},{10,9},{9,1... | collective-permute-start | bytes 1572872 | tf_op jit(solution)/shard_map/ppermute | solution.py:189
  121.9 15.0 %collective-permute-start = (bf16[16,128,128]{2,1,0:T(8,128)(2,1)S(1)}, bf16[16,128,128]{2,1,0:T(8,128)(2,1)S(1)}, u32[]{:S(2)}, u32[]{:S(2)}) collective-permute-start(bf16[16,128,128]{2,1,0:T(8,128)(2,1)S(1)} %all-to-all-done.part0), channel_id=1, source_target_pairs={{8,0},{9,1},{10,2},{11,3},{12,4},{13,5},{14,6},{15,7},{16,8},{17,9... | collective-permute-start | bytes 1572872 | tf_op jit(solution)/shard_map/ppermute | solution.py:189
  129.4 7.5 %copy-start.4 = (bf16[512,512]{1,0:T(8,128)(2,1)}, bf16[512,512]{1,0:T(8,128)(2,1)S(1)}, u32[]{:S(2)}) copy-start(bf16[512,512]{1,0:T(8,128)(2,1)S(1)} %collective-permute-done.4.other_root) | copy-start | bytes 1572868
  132.4 4.5 %copy-start.5 = (bf16[16,128,128]{2,1,0:T(8,128)(2,1)}, bf16[16,128,128]{2,1,0:T(8,128)(2,1)S(1)}, u32[]{:S(2)}) copy-start(bf16[16,128,128]{2,1,0:T(8,128)(2,1)S(1)} %collective-permute-done.2.part3) | copy-start | bytes 1572868
  134.9 2.0 %copy-start.6 = (bf16[16,128,128]{2,1,0:T(8,128)(2,1)}, bf16[16,128,128]{2,1,0:T(8,128)(2,1)S(1)}, u32[]{:S(2)}) copy-start(bf16[16,128,128]{2,1,0:T(8,128)(2,1)S(1)} %collective-permute-done.1.part2) | copy-start | bytes 1572868
  136.9 0.8 copy-start.7
Sparse Core Ops, SparseCore 0:
  79.8 55.4 all-gather.1
